TPU v7x, 32 devices: a whole 2x2x4 slice. The times are simulated.
32 devices in a mesh: dp: 2 (over x), tp: 16 (over y, z, core).
Axes of the slice: x: 2, y: 2, z: 4, core: 2. Of those that a mesh axis runs over, the one named last changes fastest.
Arguments:
- x: bfloat16 [4096, 5120], P('dp'), parts along dimension 0
- w_gate: bfloat16 [5120, 16384], P(None, 'tp')
- w_up: bfloat16 [5120, 16384], P(None, 'tp')
- w_down: bfloat16 [16384, 5120], P('tp')
Outputs:
- output: bfloat16 [4096, 5120], P('dp'), parts along dimension 0
There are 2 independent parts. A program takes and returns all parts, laid end to end along the dimension named above; an argument that names none is the same for every part.
All inputs are finite; a program needn't handle non-finite values.
Results may differ from a plain program's by a relative error of at most 0.016.
Values are sent between devices in bfloat16 or wider.
A program may use at most 2 GiB of HBM per device.

v0:
```python
import jax
import jax.numpy as jnp
from jax import lax
from jax.sharding import PartitionSpec as P


def solution(mesh):
    def step(x, w_gate, w_up, w_down):
        gate = jnp.dot(x, w_gate, preferred_element_type=jnp.float32)
        up = jnp.dot(x, w_up, preferred_element_type=jnp.float32)
        hidden = (jax.nn.silu(gate) * up).astype(jnp.bfloat16)
        term = jnp.dot(hidden, w_down, preferred_element_type=jnp.float32).astype(jnp.bfloat16)
        return lax.psum(term, "tp")

    return jax.shard_map(
        step,
        mesh=mesh,
        in_specs=(P("dp", None), P(None, "tp"), P(None, "tp"), P("tp", None)),
        out_specs=P("dp", None),
        check_vma=False,
    )
```

profile of v0, /device:TPU:0, one launch (start us, length us, event | category | flops | bytes accessed | tf_op | source)
XLA Modules:
  0.0 484.1 jit_solution(14845087773447263629)
XLA Ops:
  6.5 0.0 all-reduce.2.cloned.1.call-start
  6.5 0.0 copy-start
  6.5 29.3 %fusion = f32[2048,1024]{1,0:T(8,128)} fusion(bf16[2048,5120]{1,0:T(8,128)(2,1)} %param.4, bf16[5120,1024]{1,0:T(8,128)(2,1)} %param.5), kind=kOutput, calls=%fused_computation.2 | convolution fusion | flops 21474836480 | bytes 39845888 | tf_op jit(solution)/shard_map/dot_general | solution.py:9
  35.8 0.0 copy-done
  35.8 29.6 %multiply_convert_fusion = bf16[2048,1024]{1,0:T(8,128)(2,1)} fusion(f32[2048,1024]{1,0:T(8,128)} %fusion, bf16[2048,5120]{1,0:T(8,128)(2,1)S(1)} %copy-done, bf16[5120,1024]{1,0:T(8,128)(2,1)} %param.6), kind=kOutput, calls=%fused_computation.1 | convolution fusion | flops 21487419392 | bytes 44040192 | tf_op jit(solution)/shard_map/dot_general | solution.py:10
  65.5 29.7 %convolution_convert_fusion = bf16[2048,5120]{1,0:T(8,128)(2,1)} fusion(bf16[2048,1024]{1,0:T(8,128)(2,1)} %multiply_convert_fusion, bf16[1024,5120]{1,0:T(8,128)(2,1)} %param.7), kind=kOutput, calls=%fused_computation | convolution fusion | flops 21485322240 | bytes 35651584 | tf_op jit(solution)/shard_map/dot_general | solution.py:12
  95.2 0.0 all-reduce.2.cloned.1.call-update
  95.2 364.8 %all-reduce.2.cloned.1.call-done = bf16[2048,5120]{1,0:T(8,128)(2,1)} async-done(((bf16[2048,5120]{1,0:T(8,128)(2,1)}), bf16[2048,5120]{1,0:T(8,128)(2,1)}) %all-reduce.2.cloned.1.call-update) | async-done | bytes 20971536 | tf_op jit(solution)/shard_map/psum | solution.py:13
  460.0 17.3 %copy.6 = bf16[2048,5120]{1,0:T(8,128)(2,1)} copy(bf16[2048,5120]{1,0:T(8,128)(2,1)} %all-reduce.2.cloned.1.call-done) | data formatting | bytes 41943040
Async XLA Ops:
  6.5 453.4 %all-reduce.2.cloned.1.call-start = ((), (), s32[]{:S(2)}) async-start(), calls=%async_computation | async-start | bytes 41943040 | tf_op jit(solution)/shard_map/psum | solution.py:13
  6.5 29.3 %copy-start = (bf16[2048,5120]{1,0:T(8,128)(2,1)S(1)}, bf16[2048,5120]{1,0:T(8,128)(2,1)}, u32[]{:S(2)}) copy-start(bf16[2048,5120]{1,0:T(8,128)(2,1)} %param.4) | copy-start | bytes 62914564
Sparse Core Ops, SparseCore 0:
  95.3 364.6 all-reduce.1
where the time goes:
time: 484 us
  waiting for transfers between devices  365 us (75%)
  matrix products  88.6 us (18%)
  local copies, waits for them, and re-layouts  17.3 us (4%)
  between operations  13.4 us (3%)
    psum x1, waiting for transfers between devices, step(): return lax.psum(term, 'tp')  365 us
    dot_general x1, matrix products, step(): jnp.dot(hidden, w_down, preferred_element_type=jnp.float32)  29.7 us
    dot_general x1, matrix products, step(): up = jnp.dot(x, w_up, preferred_element_type=jnp.float32)  29.6 us
    dot_general x1, matrix products, step(): gate = jnp.dot(x, w_gate, preferred_element_type=jnp.float32)  29.3 us
    unnamed x3, local copies, waits for them, and re-layouts  17.3 us
  transfers between devices with their start and end apart: 1, of which 1 were waited for; matrix products, arithmetic and copies ran while one was open for 0% of the time, Pallas kernels for 0%

commit v1 on v0

v1 whole, which is shorter than its diff:
```python
import functools

import jax
import jax.numpy as jnp
from jax import lax
from jax.experimental import pallas as pl
from jax.experimental.pallas import tpu as pltpu
from jax.sharding import PartitionSpec as P

MESH = pl.DeviceIdType.MESH
CHIPS = 8
SUBS = 4
F32 = jnp.float32
BF16 = jnp.bfloat16


def block_kernel(x, wg, wu, wd, out, wg_v, wu_v, wd_v, xb, acc, theirs, d2d, hid,
                 w_sem, x_sem, d2d_send, d2d_recv, rs_send, rs_recv,
                 ag_send, ag_recv, pair_send, pair_recv):
    rows, depth = x.shape
    ff = wg.shape[1]
    cols = wd.shape[1]
    block = rows // CHIPS
    half = block // 2
    quarter = half // 2
    sub = quarter // SUBS
    gu_n = ff // SUBS

    tp = lax.axis_index("tp")
    core = tp % 2
    chip = tp // 2
    place = chip + (chip // 4) * (11 - 2 * chip)

    def at_place(k):
        k = k % CHIPS
        return 2 * (k + (k // 4) * (11 - 2 * k)) + core

    ring = (at_place(place + 1), at_place(place + CHIPS - 1))
    sibling = tp + 1 - 2 * core

    def block_of(d, s):
        if d == 0:
            return (place + 2 * CHIPS - 1 - s) % CHIPS
        return (place + 1 + s) % CHIPS

    def first_row(d, s, c):
        return block_of(d, s) * block + d * half + c * quarter

    def piece(d, s, j):
        return pl.ds(pl.multiple_of(first_row(d, s, core) + sub * j, sub), sub)

    def remote(src, dst, send, recv, device):
        return pltpu.make_async_remote_copy(
            src_ref=src, dst_ref=dst, send_sem=send, recv_sem=recv,
            device_id={"tp": device}, device_id_type=MESH)

    def x_copy(s, k):
        d, other = k % 2, k // 2
        c = core if other == 0 else 1 - core
        start = pl.multiple_of(first_row(d, s, c), quarter)
        return pltpu.make_async_copy(
            x.at[pl.ds(start, quarter), :], xb.at[pl.ds(k * quarter, quarter), :], x_sem.at[k])

    def w_copy(k, j):
        n = pl.ds(pl.multiple_of(j * gu_n, gu_n), gu_n)
        src, dst = ((wg, wg_v), (wu, wu_v))[k]
        return pltpu.make_async_copy(src.at[:, n], dst.at[:, n], w_sem.at[k, j])

    def wd_copy():
        return pltpu.make_async_copy(wd, wd_v, w_sem.at[2, 0])

    def d2d_copy(s):
        return remote(theirs, d2d.at[s % 2], d2d_send.at[0], d2d_recv.at[s % 2], sibling)

    def rs_copy(d, s, j):
        r = piece(d, s, j)
        return remote(out.at[r, :], out.at[r, :], rs_send.at[d, s, j], rs_recv.at[d, s, j], ring[d])

    def ag_copy(d, t, j):
        r = piece(d, t + CHIPS - 1, j)
        return remote(out.at[r, :], out.at[r, :], ag_send.at[d, t, j], ag_recv.at[d, t, j], ring[d])

    def pair_copy(d, t, j, c):
        r = pl.ds(pl.multiple_of(first_row(d, t + CHIPS - 1, c) + sub * j, sub), sub)
        return remote(out.at[r, :], out.at[r, :], pair_send.at[d, t, j], pair_recv.at[d, t, j], sibling)

    for k in range(4):
        x_copy(0, k).start()
    for j in range(SUBS):
        w_copy(0, j).start()
        w_copy(1, j).start()
    wd_copy().start()

    barrier = pltpu.get_barrier_semaphore()
    for device in (*ring, sibling):
        pl.semaphore_signal(barrier, inc=1, device_id={"tp": device}, device_id_type=MESH)
    pl.semaphore_wait(barrier, 3)

    def own_and_sibling(d, s, j):
        r = pl.ds(pl.multiple_of(d * quarter + sub * j, sub), sub)
        return acc[r, :] + d2d[s % 2, r, :].astype(F32)

    def combine(s, j):
        for d in range(2):
            rs_copy(d, s - 1, j).wait_send()
            pltpu.make_async_remote_copy(
                src_ref=out.at[piece(d, s, j), :], dst_ref=out.at[piece(d, s, j), :],
                send_sem=rs_send.at[d, s - 1, j], recv_sem=rs_recv.at[d, s - 1, j],
                device_id={"tp": ring[d]}, device_id_type=MESH).wait_recv()
            r = piece(d, s, j)
            out[r, :] = (own_and_sibling(d, s, j) + out[r, :].astype(F32)).astype(BF16)

    def comm(s, j):
        @pl.when(s == 0)
        def _():
            for d in range(2):
                out[piece(d, s, j), :] = own_and_sibling(d, s, j).astype(BF16)

        @pl.when(s > 0)
        def _():
            combine(s, j)

        for d in range(2):
            rs_copy(d, s, j).start()

    def step(i, _):
        for k in range(4):
            x_copy(i, k).wait()

        @pl.when(i > 0)
        def _():
            d2d_copy(i - 1).wait_recv()

        def gate_up(j, _):
            @pl.when(i == 0)
            def _():
                w_copy(0, j).wait()
                w_copy(1, j).wait()

            @pl.when(i > 0)
            def _():
                comm(i - 1, j)

            n = pl.ds(pl.multiple_of(j * gu_n, gu_n), gu_n)
            gate = jnp.dot(xb[...], wg_v[:, n], preferred_element_type=F32)
            up = jnp.dot(xb[...], wu_v[:, n], preferred_element_type=F32)
            hid[:, n] = (jax.nn.silu(gate) * up).astype(BF16)
            return _

        lax.fori_loop(0, SUBS, gate_up, None)

        @pl.when(i < CHIPS - 1)
        def _():
            for k in range(4):
                x_copy(i + 1, k).start()

        @pl.when(i == 0)
        def _():
            wd_copy().wait()

        @pl.when(i > 0)
        def _():
            d2d_copy(i - 1).wait_send()

        dn_n = 512

        def down(j, _):
            n = pl.ds(pl.multiple_of(j * dn_n, dn_n), dn_n)
            term = jnp.dot(hid[...], wd_v[:, n], preferred_element_type=F32)
            acc[:, n] = term[:half]
            theirs[:, n] = term[half:].astype(BF16)
            return _

        lax.fori_loop(0, cols // dn_n, down, None)
        d2d_copy(i).start()
        return _

    lax.fori_loop(0, CHIPS, step, None)

    last = CHIPS - 1
    d2d_copy(last).wait()

    def finish(j, _):
        combine(last, j)
        for d in range(2):
            ag_copy(d, 0, j).start()
            pair_copy(d, 0, j, core).start()
        return _

    lax.fori_loop(0, SUBS, finish, None)

    def gather(t, _):
        def body(j, _):
            for d in range(2):
                r = piece(d, t + CHIPS, j)
                remote(out.at[r, :], out.at[r, :], ag_send.at[d, t, j], ag_recv.at[d, t, j],
                       ring[d]).wait_recv()

                @pl.when(t < CHIPS - 2)
                def _():
                    ag_copy(d, t + 1, j).start()

                pair_copy(d, t + 1, j, core).start()
            return _

        return lax.fori_loop(0, SUBS, body, _)

    lax.fori_loop(0, CHIPS - 1, gather, None)

    def drain(t, _):
        def body(j, _):
            for d in range(2):
                @pl.when(t < CHIPS - 1)
                def _():
                    ag_copy(d, t, j).wait_send()

                pair_copy(d, t, j, core).wait_send()
                pair_copy(d, t, j, 1 - core).wait_recv()
            return _

        return lax.fori_loop(0, SUBS, body, _)

    lax.fori_loop(0, CHIPS, drain, None)


def copy_out_kernel(parts, src, dst, sem):
    n = src.shape[0] // parts
    copies = [
        pltpu.make_async_copy(src.at[pl.ds(k * n, n), :], dst.at[pl.ds(k * n, n), :], sem.at[k])
        for k in range(parts)
    ]
    for copy in copies:
        copy.start()
    for copy in copies:
        copy.wait()


def mlp(x, w_gate, w_up, w_down):
    rows, depth = x.shape
    ff = w_gate.shape[1]
    cols = w_down.shape[1]
    block = rows // CHIPS
    half = block // 2
    dma = pltpu.SemaphoreType.DMA
    any_spec = pl.BlockSpec(memory_space=pl.ANY)
    flops = 6 * rows * depth * ff
    y = pl.pallas_call(
        block_kernel,
        out_shape=pltpu.VMEM((rows, cols), BF16),
        in_specs=[any_spec] * 4,
        out_specs=pl.BlockSpec(memory_space=pltpu.VMEM),
        scratch_shapes=[
            pltpu.VMEM((depth, ff), BF16),
            pltpu.VMEM((depth, ff), BF16),
            pltpu.VMEM((ff, cols), BF16),
            pltpu.VMEM((block, depth), BF16),
            pltpu.VMEM((half, cols), F32),
            pltpu.VMEM((half, cols), BF16),
            pltpu.VMEM((2, half, cols), BF16),
            pltpu.VMEM((block, ff), BF16),
            dma((3, SUBS)),
            dma((4,)),
            dma((1,)),
            dma((2,)),
            dma((2, CHIPS - 1, SUBS)),
            dma((2, CHIPS - 1, SUBS)),
            dma((2, CHIPS - 1, SUBS)),
            dma((2, CHIPS - 1, SUBS)),
            dma((2, CHIPS, SUBS)),
            dma((2, CHIPS, SUBS)),
        ],
        compiler_params=pltpu.CompilerParams(
            collective_id=0, has_side_effects=True, vmem_limit_bytes=43 * 2**20),
        cost_estimate=pl.CostEstimate(
            flops=flops, bytes_accessed=2 * (rows * depth + 3 * depth * ff), transcendentals=rows * ff),
        name="mlp_ring",
    )(x, w_gate, w_up, w_down)
    parts = 16
    return pl.pallas_call(
        functools.partial(copy_out_kernel, parts),
        out_shape=jax.ShapeDtypeStruct((rows, cols), BF16),
        in_specs=[pl.BlockSpec(memory_space=pltpu.VMEM)],
        out_specs=any_spec,
        scratch_shapes=[dma((parts,))],
        compiler_params=pltpu.CompilerParams(vmem_limit_bytes=2**20),
        name="copy_out",
    )(y)


def solution(mesh):
    return jax.shard_map(
        mlp,
        mesh=mesh,
        in_specs=(P("dp", None), P(None, "tp"), P(None, "tp"), P("tp", None)),
        out_specs=P("dp", None),
        check_vma=False,
    )
```

time: 484 us -> 235 us (0.49)
  waiting for transfers between devices: 365 us -> 0 us
  Pallas kernels: 0 us -> 235 us
  matrix products: 88.6 us -> 0 us
  local copies, waits for them, and re-layouts: 17.3 us -> 0 us
  between operations: 13.4 us -> 0.01 us
    psum x1 -> x0, waiting for transfers between devices: 365 us -> none  [step(): return lax.psum(term, 'tp')]
    pallas_call x0 -> x2, Pallas kernels: none -> 235 us  [the longest x1 228 us: mlp(): pl.pallas_call(block_kernel, out_shape=pltpu.VMEM((rows, cols), BF16), in...]
    dot_general x3 -> x0, matrix products: 88.6 us -> none  [the longest x1 29.7 us: step(): jnp.dot(hidden, w_down, preferred_element_type=jnp.float32)]
    unnamed x3 -> x0, local copies, waits for them, and re-layouts: 17.3 us -> none
  transfers between devices with their start and end apart: 1 -> 0, of which waited for: 1 -> 0; matrix products, arithmetic and copies ran while one was open for 0% -> 0% of each run, Pallas kernels for 0% -> 0%
where the time goes in v1:
time: 235 us
  Pallas kernels  235 us (100%)
    pallas_call x1, Pallas kernels, mlp(): pl.pallas_call(block_kernel, out_shape=pltpu.VMEM((rows, cols), BF16), in...  228 us
    pallas_call x1, Pallas kernels, mlp(): pl.pallas_call(functools.partial(copy_out_kernel, parts), out_shape=jax.S...  7.26 us

profile of v1, /device:TPU:0, one launch (start us, length us, event | category | flops | bytes accessed | tf_op | source)
XLA Modules:
  0.0 235.1 jit_solution(12754839305151156919)
XLA Ops:
  0.0 227.8 %mlp_ring.1.src = bf16[2048,5120]{1,0:T(8,128)(2,1)S(1)} custom-call(bf16[2048,5120]{1,0:T(8,128)(2,1)} %x.1, bf16[5120,1024]{1,0:T(8,128)(2,1)} %wg.1, bf16[5120,1024]{1,0:T(8,128)(2,1)} %wu.1, bf16[1024,5120]{1,0:T(8,128)(2,1)} %wd.1), custom_call_target="tpu_custom_call" | custom-call | flops 64424509440 | bytes 52428800 | tf_op jit(solution)/shard_map/mlp_ring/pallas_call | solution.py:247
  227.8 7.3 %copy_out.1 = bf16[2048,5120]{1,0:T(8,128)(2,1)} custom-call(bf16[2048,5120]{1,0:T(8,128)(2,1)S(1)} %mlp_ring.1.src), custom_call_target="tpu_custom_call" | custom-call | tf_op jit(solution)/shard_map/copy_out/pallas_call | solution.py:279

commit v2 on v0

v2 whole, which is shorter than its diff:
```python
import functools

import jax
import jax.numpy as jnp
from jax import lax
from jax.experimental import pallas as pl
from jax.experimental.pallas import tpu as pltpu
from jax.sharding import PartitionSpec as P

MESH = pl.DeviceIdType.MESH
F32 = jnp.float32
BF16 = jnp.bfloat16

ROUNDS = 25
TREES = (
    (2, (2, 0, -1, 2, 2, 4, 4, 6), (15, 6, -1, 17, 18, 9, 17, 5), (19, 20, -1, 22, 19, 21, 20, 21)),
    (0, (-1, 0, 4, 1, 6, 3, 7, 5), (-1, 7, 0, 6, 1, 4, 2, 3), (-1, 8, 23, 9, 22, 10, 15, 11)),
    (0, (-1, 0, 3, 1, 2, 3, 7, 5), (-1, 9, 3, 7, 1, 6, 4, 5), (-1, 10, 20, 19, 24, 21, 23, 22)),
    (2, (2, 3, -1, 2, 6, 3, 7, 5), (12, 11, -1, 12, 2, 5, 3, 4), (13, 14, -1, 13, 20, 14, 16, 15)),
    (0, (-1, 3, 0, 2, 6, 3, 7, 5), (-1, 1, 5, 4, 0, 3, 1, 2), (-1, 8, 6, 7, 21, 8, 11, 9)),
    (0, (-1, 3, 0, 2, 2, 4, 4, 6), (-1, 10, 12, 11, 11, 2, 8, 0), (-1, 24, 13, 15, 15, 16, 16, 17)),
    (0, (-1, 0, 0, 2, 2, 3, 4, 5), (-1, 14, 10, 8, 9, 7, 7, 0), (-1, 18, 18, 19, 22, 20, 23, 21)),
    (2, (2, 0, -1, 2, 2, 4, 4, 6), (16, 12, -1, 14, 16, 10, 14, 13), (17, 19, -1, 18, 17, 23, 18, 22)),
)
NODES = range(8)
SUBS = 2
SLOT = 2


def outer(v):
    return v // 2 in (0, 3)


def children(b, v):
    _, parent, up, _ = TREES[b]
    return sorted((c for c in NODES if parent[c] == v), key=lambda c: up[c])


def use_round(b, v):
    root, _, up, _ = TREES[b]
    return max(up[c] for c in children(b, v)) + 1 if v == root else up[v]


def plan_steps(is_outer):
    items = sorted((use_round(b, v), b, v) for b in range(len(TREES)) for v in NODES if outer(v) == is_outer)
    steps = {}
    for use, b, v in reversed(items):
        if not steps or len(steps[min(steps)]) == SLOT:
            step = min([use, *(s - 1 for s in steps)])
        else:
            step = min(use, min(steps))
        assert step == use
        steps.setdefault(step, []).append((b, v))
    assert min(steps) >= 0
    return {s: sorted(units) for s, units in steps.items()}


def port_of(v, w):
    if v // 2 == w // 2:
        return 0
    return 1 if outer(v) or outer(w) else 2


STEPS = {o: plan_steps(o) for o in (True, False)}
EXTRA = {}
for _o in (True, False):
    _found = [(b, v, c) for b in range(len(TREES)) for v in NODES if outer(v) == _o for c in children(b, v)[1:]]
    EXTRA.update({key: k for k, key in enumerate(_found)})
N_EXTRA = max(EXTRA.values()) + 1
SENDS = {(o, e): [] for o in (True, False) for e in range(3)}
for _b, (_root, _parent, _up, _down) in enumerate(TREES):
    for _v in NODES:
        if _v != _root:
            SENDS[outer(_v), port_of(_v, _parent[_v])].append(_up[_v])
            SENDS[outer(_parent[_v]), port_of(_v, _parent[_v])].append(_down[_v])
assert all(len(set(rounds)) == len(rounds) for rounds in SENDS.values())


def select(index, values):
    out = jnp.int32(values[0])
    for k, value in enumerate(values):
        if k:
            out = jnp.where(index == k, jnp.int32(value), out)
    return out


def block_kernel(x, wg, wu, wd, out, wg_v, wu_v, wd_v, xb, acc, theirs, d2d, hid, stage, extra,
                 w_sem, x_sem, d2d_send, d2d_recv, send_sem, rs_recv, extra_recv, ag_recv, pair_send, pair_recv):
    rows = x.shape[0]
    cols = wd.shape[1]
    n_units = 4 * len(TREES)
    unit = rows // n_units
    half = unit // 2
    sub = half // SUBS

    tp = lax.axis_index("tp")
    core = tp % 2
    z = (tp // 2) % 4
    y = tp // 8
    far = z // 2
    nz = z + far * (3 - 2 * z)
    is_outer = nz == 0
    is_inner = nz == 1
    toward = 1 - 2 * far

    def device(yy, zz):
        return (yy * 4 + zz) * 2 + core

    sibling = tp + 1 - 2 * core
    ports = {
        True: (device(1 - y, z), device(y, z + toward)),
        False: (device(1 - y, z), device(y, z - toward), device(y, z + toward)),
    }

    def code(b, v):
        return 4 * b + 2 * (v % 2) + (v // 2) // 2

    def image(q):
        return 4 * (q // 4) + 2 * (((q // 2) % 2 + y) % 2) + (q % 2 + far) % 2

    def piece(u, j, c=None):
        return pl.ds(pl.multiple_of(u * unit + (core if c is None else c) * half + sub * j, sub), sub)

    def remote(src, dst, send, recv, to):
        return pltpu.make_async_remote_copy(
            src_ref=src, dst_ref=dst, send_sem=send, recv_sem=recv,
            device_id={"tp": to}, device_id_type=MESH)

    def landing(b, v, c, u, j):
        if children(b, v)[0] == c:
            return out.at[piece(u, j), :], rs_recv.at[u, j]
        k = EXTRA[b, v, c]
        return extra.at[k, pl.ds(pl.multiple_of(sub * j, sub), sub), :], extra_recv.at[k, j]

    def pair_copy(u, j, c=None):
        r = piece(u, j, c)
        return remote(out.at[r, :], out.at[r, :], pair_send.at[u, j], pair_recv.at[u, j], sibling)

    def d2d_copy(s):
        return remote(theirs, d2d.at[s % 2], d2d_send.at[0], d2d_recv.at[s % 2], sibling)

    n_steps = jnp.where(is_outer, max(STEPS[True]) + 1, max(STEPS[False]) + 1)
    most = max(max(STEPS[True]), max(STEPS[False])) + 1

    def step_units(s):
        picked = []
        for k in range(SLOT):
            q = {}
            for o in (True, False):
                table = []
                for i in range(most):
                    items = STEPS[o].get(i, [(0, 0 if o else 2)])
                    b, v = items[min(k, len(items) - 1)]
                    table.append(code(b, v))
                q[o] = select(s, table)
            picked.append(image(jnp.where(is_outer, q[True], q[False])))
        return picked

    def x_copies(s):
        copies = []
        units = step_units(s)
        for other in range(2):
            c = core + other * (1 - 2 * core)
            for k in range(SLOT):
                n = other * SLOT + k
                start = pl.multiple_of(units[k] * unit + c * half, half)
                copies.append(pltpu.make_async_copy(
                    x.at[pl.ds(start, half), :], xb.at[pl.ds(n * half, half), :], x_sem.at[n]))
        return copies

    w_copies = [
        pltpu.make_async_copy(wg, wg_v, w_sem.at[0]),
        pltpu.make_async_copy(wu, wu_v, w_sem.at[1]),
        pltpu.make_async_copy(wd, wd_v, w_sem.at[2]),
    ]
    for copy in x_copies(jnp.int32(0)) + w_copies:
        copy.start()

    barrier = pltpu.get_barrier_semaphore()
    for o, here in ((True, is_outer), (False, is_inner)):
        @pl.when(here)
        def _(o=o):
            for to in (*ports[o], sibling):
                pl.semaphore_signal(barrier, inc=1, device_id={"tp": to}, device_id_type=MESH)
            pl.semaphore_wait(barrier, len(ports[o]) + 1)

    def send(o, e, r, j, src, dst, recv):
        remote(src, dst, send_sem.at[e, r % 2, j], recv, ports[o][e]).start()

    def free_slot(o, e, r, j):
        if any(k < r and (r - k) % 2 == 0 for k in SENDS[o, e]):
            slot = stage.at[e, r % 2, j]
            remote(slot, slot, send_sem.at[e, r % 2, j], ag_recv.at[0, 0], ports[o][e]).wait_send()

    def total(o, b, v, u, j, store):
        use = use_round(b, v)
        k = STEPS[o][use].index((b, v))
        r = pl.ds(pl.multiple_of(k * half + sub * j, sub), sub)
        places = []
        for c in children(b, v):
            ref, sem = landing(b, v, c, u, j)
            remote(ref, ref, send_sem.at[0, 0, 0], sem, sibling).wait_recv()
            places.append(ref)
        value = acc[r, :] + d2d[use % 2, r, :].astype(F32)
        for ref in places:
            value = value + ref[...].astype(F32)
        store[...] = value.astype(BF16)

    def comm(o, r, j):
        nodes = [(b, v) for b in range(len(TREES)) for v in NODES if outer(v) == o]
        for b, v in nodes:
            root, parent, up, down = TREES[b]
            if v != root and down[v] == r - 1:
                u = image(code(b, v))
                mine = out.at[piece(u, j), :]
                remote(mine, mine, send_sem.at[0, 0, 0], ag_recv.at[u, j], sibling).wait_recv()
                pair_copy(u, j).start()
        for b, v in nodes:
            if v == TREES[b][0] and use_round(b, v) == r:
                u = image(code(b, v))
                total(o, b, v, u, j, out.at[piece(u, j), :])
                pair_copy(u, j).start()
        for b, v in nodes:
            root, parent, up, down = TREES[b]
            for w in children(b, v):
                if down[w] == r:
                    u = image(code(b, v))
                    e = port_of(v, w)
                    free_slot(o, e, r, j)
                    r_out = out.at[piece(u, j), :]
                    send(o, e, r, j, r_out, r_out, ag_recv.at[u, j])
            if v != root and up[v] == r:
                u = image(code(b, v))
                e = port_of(v, parent[v])
                free_slot(o, e, r, j)
                slot = stage.at[e, r % 2, j]
                total(o, b, v, u, j, slot)
                send(o, e, r, j, slot, *landing(b, parent[v], v, u, j))

    def gate_up(s):
        for copy in x_copies(s):
            copy.wait()

        @pl.when(s == 0)
        def _():
            w_copies[0].wait()
            w_copies[1].wait()

        gate = jnp.dot(xb[...], wg_v[...], preferred_element_type=F32)
        up = jnp.dot(xb[...], wu_v[...], preferred_element_type=F32)
        hid[...] = (jax.nn.silu(gate) * up).astype(BF16)

        @pl.when(s + 1 < n_steps)
        def _():
            for copy in x_copies(s + 1):
                copy.start()

    def down_proj(s):
        @pl.when(s == 0)
        def _():
            w_copies[2].wait()

        @pl.when(s > 0)
        def _():
            d2d_copy(s - 1).wait_send()

        n_cols = cols // 2

        def part(k, carry):
            n = pl.ds(pl.multiple_of(k * n_cols, n_cols), n_cols)
            term = jnp.dot(hid[...], wd_v[:, n], preferred_element_type=F32)
            acc[:, n] = term[:SLOT * half]
            theirs[:, n] = term[SLOT * half:].astype(BF16)
            return carry

        lax.fori_loop(0, cols // n_cols, part, None)
        d2d_copy(s).start()

    def round_(i, carry):
        r = i - 1
        s = r + 1

        @pl.when((r >= 0) & (r < n_steps))
        def _():
            d2d_copy(r).wait_recv()

        def body(j, carry):
            for o, here in ((True, is_outer), (False, is_inner)):
                @pl.when(here)
                def _(o=o):
                    for k in range(ROUNDS + 1):
                        @pl.when(r == k)
                        def _(k=k):
                            comm(o, k, j)

            @pl.when((s < n_steps) & (j == 0))
            def _():
                gate_up(s)

            @pl.when((s < n_steps) & (j == SUBS - 1))
            def _():
                down_proj(s)

            return carry

        return lax.fori_loop(0, SUBS, body, carry)

    lax.fori_loop(0, ROUNDS + 2, round_, None)

    for o, here in ((True, is_outer), (False, is_inner)):
        @pl.when(here)
        def _(o=o):
            for e in range(len(ports[o])):
                for parity in sorted({r % 2 for r in SENDS[o, e]}):
                    for j in range(SUBS):
                        slot = stage.at[e, parity, j]
                        remote(slot, slot, send_sem.at[e, parity, j], ag_recv.at[0, 0], ports[o][e]).wait_send()

    d2d_copy(n_steps - 1).wait_send()

    def drain(u, carry):
        for j in range(SUBS):
            pair_copy(u, j).wait_send()
            pair_copy(u, j, 1 - core).wait_recv()
        return carry

    lax.fori_loop(0, n_units, drain, None)


def copy_out_kernel(parts, src, dst, sem):
    n = src.shape[0] // parts
    copies = [
        pltpu.make_async_copy(src.at[pl.ds(k * n, n), :], dst.at[pl.ds(k * n, n), :], sem.at[k])
        for k in range(parts)
    ]
    for copy in copies:
        copy.start()
    for copy in copies:
        copy.wait()


def mlp(x, w_gate, w_up, w_down):
    rows, depth = x.shape
    ff = w_gate.shape[1]
    cols = w_down.shape[1]
    n_units = 4 * len(TREES)
    half = rows // n_units // 2
    sub = half // SUBS
    dma = pltpu.SemaphoreType.DMA
    any_spec = pl.BlockSpec(memory_space=pl.ANY)
    y = pl.pallas_call(
        block_kernel,
        out_shape=pltpu.VMEM((rows, cols), BF16),
        in_specs=[any_spec] * 4,
        out_specs=pl.BlockSpec(memory_space=pltpu.VMEM),
        scratch_shapes=[
            pltpu.VMEM((depth, ff), BF16),
            pltpu.VMEM((depth, ff), BF16),
            pltpu.VMEM((ff, cols), BF16),
            pltpu.VMEM((2 * SLOT * half, depth), BF16),
            pltpu.VMEM((SLOT * half, cols), F32),
            pltpu.VMEM((SLOT * half, cols), BF16),
            pltpu.VMEM((2, SLOT * half, cols), BF16),
            pltpu.VMEM((2 * SLOT * half, ff), BF16),
            pltpu.VMEM((3, 2, SUBS, sub, cols), BF16),
            pltpu.VMEM((N_EXTRA, half, cols), BF16),
            dma((3,)),
            dma((2 * SLOT,)),
            dma((1,)),
            dma((2,)),
            dma((3, 2, SUBS)),
            dma((n_units, SUBS)),
            dma((N_EXTRA, SUBS)),
            dma((n_units, SUBS)),
            dma((n_units, SUBS)),
            dma((n_units, SUBS)),
        ],
        compiler_params=pltpu.CompilerParams(
            collective_id=0, has_side_effects=True, vmem_limit_bytes=43 * 2**20),
        cost_estimate=pl.CostEstimate(
            flops=6 * rows * depth * ff, bytes_accessed=2 * (rows * depth + 3 * depth * ff),
            transcendentals=rows * ff),
        name="mlp_trees",
    )(x, w_gate, w_up, w_down)
    parts = 16
    return pl.pallas_call(
        functools.partial(copy_out_kernel, parts),
        out_shape=jax.ShapeDtypeStruct((rows, cols), BF16),
        in_specs=[pl.BlockSpec(memory_space=pltpu.VMEM)],
        out_specs=any_spec,
        scratch_shapes=[dma((parts,))],
        compiler_params=pltpu.CompilerParams(vmem_limit_bytes=2**20),
        name="copy_out",
    )(y)


def solution(mesh):
    return jax.shard_map(
        mlp,
        mesh=mesh,
        in_specs=(P("dp", None), P(None, "tp"), P(None, "tp"), P("tp", None)),
        out_specs=P("dp", None),
        check_vma=False,
    )
```

time: 484 us -> 209 us (0.43)
  waiting for transfers between devices: 365 us -> 0 us
  Pallas kernels: 0 us -> 208 us
  matrix products: 88.6 us -> 0 us
  local copies, waits for them, and re-layouts: 17.3 us -> 0 us
  between operations: 13.4 us -> 0.01 us
    psum x1 -> x0, waiting for transfers between devices: 365 us -> none  [step(): return lax.psum(term, 'tp')]
    pallas_call x0 -> x2, Pallas kernels: none -> 208 us  [the longest x1 201 us: mlp(): pl.pallas_call(block_kernel, out_shape=pltpu.VMEM((rows, cols), BF16), in...]
    dot_general x3 -> x0, matrix products: 88.6 us -> none  [the longest x1 29.7 us: step(): jnp.dot(hidden, w_down, preferred_element_type=jnp.float32)]
    unnamed x3 -> x0, local copies, waits for them, and re-layouts: 17.3 us -> none
  transfers between devices with their start and end apart: 1 -> 0, of which waited for: 1 -> 0; matrix products, arithmetic and copies ran while one was open for 0% -> 0% of each run, Pallas kernels for 0% -> 0%
where the time goes in v2:
time: 209 us; the launch traced here: 208 us
  Pallas kernels  208 us (100%)
    pallas_call x1, Pallas kernels, mlp(): pl.pallas_call(block_kernel, out_shape=pltpu.VMEM((rows, cols), BF16), in...  201 us
    pallas_call x1, Pallas kernels, mlp(): pl.pallas_call(functools.partial(copy_out_kernel, parts), out_shape=jax.S...  7.26 us

profile of v2, /device:TPU:0, one launch (start us, length us, event | category | flops | bytes accessed | tf_op | source)
XLA Modules:
  0.0 208.4 jit_solution(3636567742737400939)
XLA Ops:
  0.0 201.1 %mlp_trees.1.src = bf16[2048,5120]{1,0:T(8,128)(2,1)S(1)} custom-call(bf16[2048,5120]{1,0:T(8,128)(2,1)} %x.1, bf16[5120,1024]{1,0:T(8,128)(2,1)} %wg.1, bf16[5120,1024]{1,0:T(8,128)(2,1)} %wu.1, bf16[1024,5120]{1,0:T(8,128)(2,1)} %wd.1), custom_call_target="tpu_custom_call" | custom-call | flops 64424509440 | bytes 52428800 | tf_op jit(solution)/shard_map/mlp_trees/pallas_call | solution.py:351
  201.1 7.3 %copy_out.1 = bf16[2048,5120]{1,0:T(8,128)(2,1)} custom-call(bf16[2048,5120]{1,0:T(8,128)(2,1)S(1)} %mlp_trees.1.src), custom_call_target="tpu_custom_call" | custom-call | tf_op jit(solution)/shard_map/copy_out/pallas_call | solution.py:386

commit v3 on v2

--- a/solution.py
+++ b/solution.py
@@ -11,20 +11,23 @@
 F32 = jnp.float32
 BF16 = jnp.bfloat16
 
-ROUNDS = 25
+ROUNDS = 24
 TREES = (
-    (2, (2, 0, -1, 2, 2, 4, 4, 6), (15, 6, -1, 17, 18, 9, 17, 5), (19, 20, -1, 22, 19, 21, 20, 21)),
-    (0, (-1, 0, 4, 1, 6, 3, 7, 5), (-1, 7, 0, 6, 1, 4, 2, 3), (-1, 8, 23, 9, 22, 10, 15, 11)),
-    (0, (-1, 0, 3, 1, 2, 3, 7, 5), (-1, 9, 3, 7, 1, 6, 4, 5), (-1, 10, 20, 19, 24, 21, 23, 22)),
-    (2, (2, 3, -1, 2, 6, 3, 7, 5), (12, 11, -1, 12, 2, 5, 3, 4), (13, 14, -1, 13, 20, 14, 16, 15)),
-    (0, (-1, 3, 0, 2, 6, 3, 7, 5), (-1, 1, 5, 4, 0, 3, 1, 2), (-1, 8, 6, 7, 21, 8, 11, 9)),
-    (0, (-1, 3, 0, 2, 2, 4, 4, 6), (-1, 10, 12, 11, 11, 2, 8, 0), (-1, 24, 13, 15, 15, 16, 16, 17)),
-    (0, (-1, 0, 0, 2, 2, 3, 4, 5), (-1, 14, 10, 8, 9, 7, 7, 0), (-1, 18, 18, 19, 22, 20, 23, 21)),
-    (2, (2, 0, -1, 2, 2, 4, 4, 6), (16, 12, -1, 14, 16, 10, 14, 13), (17, 19, -1, 18, 17, 23, 18, 22)),
+    (0, (-1, 0, 0, 2, 2, 4, 4, 6), (-1, 9, 13, 9, 12, 8, 11, 4), (-1, 15, 14, 19, 15, 18, 16, 17)),
+    (0, (-1, 3, 0, 5, 2, 4, 4, 5), (-1, 8, 14, 10, 13, 11, 12, 10), (-1, 23, 15, 19, 16, 17, 17, 20)),
+    (0, (-1, 0, 0, 2, 2, 4, 4, 6), (-1, 16, 19, 14, 18, 12, 17, 1), (-1, 21, 20, 21, 21, 23, 22, 23)),
+    (0, (-1, 3, 0, 2, 2, 3, 4, 5), (-1, 1, 4, 3, 3, 2, 2, 0), (-1, 8, 5, 6, 6, 9, 7, 11)),
+    (0, (-1, 0, 3, 1, 6, 3, 7, 5), (-1, 10, 7, 9, 0, 7, 5, 6), (-1, 12, 15, 13, 21, 14, 18, 15)),
+    (0, (-1, 0, 0, 2, 2, 4, 4, 6), (-1, 13, 18, 10, 17, 16, 16, 0), (-1, 20, 19, 20, 20, 22, 21, 22)),
+    (0, (-1, 0, 0, 5, 2, 7, 4, 6), (-1, 6, 5, 0, 4, 1, 3, 2), (-1, 14, 7, 23, 8, 18, 10, 11)),
+    (0, (-1, 0, 3, 1, 6, 3, 7, 5), (-1, 7, 1, 6, 2, 5, 3, 4), (-1, 8, 13, 9, 23, 11, 19, 12)),
 )
 NODES = range(8)
+GROUP = 5
 SUBS = 2
 SLOT = 2
+AHEAD = 3
+PIECES = 4
 
 
 def outer(v):
@@ -156,25 +159,42 @@
             picked.append(image(jnp.where(is_outer, q[True], q[False])))
         return picked
 
+    def x_copy(start, n):
+        return pltpu.make_async_copy(
+            x.at[pl.ds(start, half), :], xb.at[pl.ds(n * half, half), :], x_sem.at[n])
+
     def x_copies(s):
+        units = step_units(s)
         copies = []
-        units = step_units(s)
-        for other in range(2):
-            c = core + other * (1 - 2 * core)
-            for k in range(SLOT):
-                n = other * SLOT + k
-                start = pl.multiple_of(units[k] * unit + c * half, half)
-                copies.append(pltpu.make_async_copy(
-                    x.at[pl.ds(start, half), :], xb.at[pl.ds(n * half, half), :], x_sem.at[n]))
+        for n in range(2 * SLOT):
+            c = core if n < SLOT else 1 - core
+            copies.append(x_copy(pl.multiple_of(units[n % SLOT] * unit + c * half, half), n))
         return copies
 
-    w_copies = [
-        pltpu.make_async_copy(wg, wg_v, w_sem.at[0]),
-        pltpu.make_async_copy(wu, wu_v, w_sem.at[1]),
-        pltpu.make_async_copy(wd, wd_v, w_sem.at[2]),
-    ]
-    for copy in x_copies(jnp.int32(0)) + w_copies:
+    g_cols = wg.shape[1] // PIECES
+    d_cols = cols // PIECES
+
+    def w_copy(i, k):
+        width = d_cols if i == 2 else g_cols
+        n = pl.ds(pl.multiple_of(k * width, width), width)
+        src, dst = ((wg, wg_v), (wu, wu_v), (wd, wd_v))[i]
+        return pltpu.make_async_copy(src.at[:, n], dst.at[:, n], w_sem.at[i, k])
+
+    def load(k):
+        @pl.when(k < PIECES)
+        def _():
+            w_copy(0, k).start()
+            w_copy(1, k).start()
+
+        @pl.when((k >= PIECES) & (2 * (k - PIECES) < PIECES))
+        def _():
+            w_copy(2, 2 * (k - PIECES)).start()
+            w_copy(2, 2 * (k - PIECES) + 1).start()
+
+    for copy in x_copies(jnp.int32(0)):
         copy.start()
+    for k in range(AHEAD):
+        load(jnp.int32(k))
 
     barrier = pltpu.get_barrier_semaphore()
     for o, here in ((True, is_outer), (False, is_inner)):
@@ -238,17 +258,28 @@
                 send(o, e, r, j, slot, *landing(b, parent[v], v, u, j))
 
     def gate_up(s):
-        for copy in x_copies(s):
-            copy.wait()
+        for n in range(2 * SLOT):
+            x_copy(0, n).wait()
+
+        def hidden(n):
+            gate = jnp.dot(xb[...], wg_v[:, n], preferred_element_type=F32)
+            up = jnp.dot(xb[...], wu_v[:, n], preferred_element_type=F32)
+            hid[:, n] = (jax.nn.silu(gate) * up).astype(BF16)
 
         @pl.when(s == 0)
         def _():
-            w_copies[0].wait()
-            w_copies[1].wait()
-
-        gate = jnp.dot(xb[...], wg_v[...], preferred_element_type=F32)
-        up = jnp.dot(xb[...], wu_v[...], preferred_element_type=F32)
-        hid[...] = (jax.nn.silu(gate) * up).astype(BF16)
+            def part(k, carry):
+                w_copy(0, k).wait()
+                w_copy(1, k).wait()
+                load(k + AHEAD)
+                hidden(pl.ds(pl.multiple_of(k * g_cols, g_cols), g_cols))
+                return carry
+
+            lax.fori_loop(0, PIECES, part, None)
+
+        @pl.when(s > 0)
+        def _():
+            hidden(slice(None))
 
         @pl.when(s + 1 < n_steps)
         def _():
@@ -256,24 +287,31 @@
                 copy.start()
 
     def down_proj(s):
+        def term(n):
+            value = jnp.dot(hid[...], wd_v[:, n], preferred_element_type=F32)
+            acc[:, n] = value[:SLOT * half]
+            theirs[:, n] = value[SLOT * half:].astype(BF16)
+
         @pl.when(s == 0)
         def _():
-            w_copies[2].wait()
+            def part(k, carry):
+                w_copy(2, k).wait()
+                term(pl.ds(pl.multiple_of(k * d_cols, d_cols), d_cols))
+                return carry
+
+            lax.fori_loop(0, PIECES, part, None)
 
         @pl.when(s > 0)
         def _():
             d2d_copy(s - 1).wait_send()
-
-        n_cols = cols // 2
-
-        def part(k, carry):
-            n = pl.ds(pl.multiple_of(k * n_cols, n_cols), n_cols)
-            term = jnp.dot(hid[...], wd_v[:, n], preferred_element_type=F32)
-            acc[:, n] = term[:SLOT * half]
-            theirs[:, n] = term[SLOT * half:].astype(BF16)
-            return carry
-
-        lax.fori_loop(0, cols // n_cols, part, None)
+            n_cols = cols
+
+            def part(k, carry):
+                term(pl.ds(pl.multiple_of(k * n_cols, n_cols), n_cols))
+                return carry
+
+            lax.fori_loop(0, cols // n_cols, part, None)
+
         d2d_copy(s).start()
 
     def round_(i, carry):
@@ -288,10 +326,13 @@
             for o, here in ((True, is_outer), (False, is_inner)):
                 @pl.when(here)
                 def _(o=o):
-                    for k in range(ROUNDS + 1):
-                        @pl.when(r == k)
-                        def _(k=k):
-                            comm(o, k, j)
+                    for first in range(0, ROUNDS + 1, GROUP):
+                        @pl.when((r >= first) & (r < first + GROUP))
+                        def _(first=first):
+                            for k in range(first, min(first + GROUP, ROUNDS + 1)):
+                                @pl.when(r == k)
+                                def _(k=k):
+                                    comm(o, k, j)
 
             @pl.when((s < n_steps) & (j == 0))
             def _():
@@ -364,7 +405,7 @@
             pltpu.VMEM((2 * SLOT * half, ff), BF16),
             pltpu.VMEM((3, 2, SUBS, sub, cols), BF16),
             pltpu.VMEM((N_EXTRA, half, cols), BF16),
-            dma((3,)),
+            dma((3, PIECES)),
             dma((2 * SLOT,)),
             dma((1,)),
             dma((2,)),
@@ -382,7 +423,7 @@
             transcendentals=rows * ff),
         name="mlp_trees",
     )(x, w_gate, w_up, w_down)
-    parts = 16
+    parts = 8
     return pl.pallas_call(
         functools.partial(copy_out_kernel, parts),
         out_shape=jax.ShapeDtypeStruct((rows, cols), BF16),

time: 209 us -> 197 us (0.943)
  Pallas kernels: 208 us -> 197 us
    pallas_call x1, Pallas kernels: 201 us -> 190 us  [mlp(): pl.pallas_call(block_kernel, out_shape=pltpu.VMEM((rows, cols), BF16), in...]
where the time goes in v3:
time: 197 us
  Pallas kernels  197 us (100%)
    pallas_call x1, Pallas kernels, mlp(): pl.pallas_call(block_kernel, out_shape=pltpu.VMEM((rows, cols), BF16), in...  190 us
    pallas_call x1, Pallas kernels, mlp(): pl.pallas_call(functools.partial(copy_out_kernel, parts), out_shape=jax.S...  7.23 us

profile of v3, /device:TPU:0, one launch (start us, length us, event | category | flops | bytes accessed | tf_op | source)
XLA Modules:
  0.0 197.3 jit_solution(12320981041071600853)
XLA Ops:
  0.0 190.1 %mlp_trees.1.src = bf16[2048,5120]{1,0:T(8,128)(2,1)S(1)} custom-call(bf16[2048,5120]{1,0:T(8,128)(2,1)} %x.1, bf16[5120,1024]{1,0:T(8,128)(2,1)} %wg.1, bf16[5120,1024]{1,0:T(8,128)(2,1)} %wu.1, bf16[1024,5120]{1,0:T(8,128)(2,1)} %wd.1), custom_call_target="tpu_custom_call" | custom-call | flops 64424509440 | bytes 52428800 | tf_op jit(solution)/shard_map/mlp_trees/pallas_call | solution.py:392
  190.1 7.2 %copy_out.1 = bf16[2048,5120]{1,0:T(8,128)(2,1)} custom-call(bf16[2048,5120]{1,0:T(8,128)(2,1)S(1)} %mlp_trees.1.src), custom_call_target="tpu_custom_call" | custom-call | tf_op jit(solution)/shard_map/copy_out/pallas_call | solution.py:427

commit v4 on v3

--- a/solution.py
+++ b/solution.py
@@ -88,7 +88,7 @@
 
 
 def block_kernel(x, wg, wu, wd, out, wg_v, wu_v, wd_v, xb, acc, theirs, d2d, hid, stage, extra,
-                 w_sem, x_sem, d2d_send, d2d_recv, send_sem, rs_recv, extra_recv, ag_recv, pair_send, pair_recv):
+                 w_sem, x_sem, first_send, first_recv, d2d_send, d2d_recv, send_sem, rs_recv, extra_recv, ag_recv, pair_send, pair_recv):
     rows = x.shape[0]
     cols = wd.shape[1]
     n_units = 4 * len(TREES)
@@ -141,6 +141,10 @@
 
     def d2d_copy(s):
         return remote(theirs, d2d.at[s % 2], d2d_send.at[0], d2d_recv.at[s % 2], sibling)
+
+    def first_copy(k):
+        n = pl.ds(pl.multiple_of(k * (cols // PIECES), cols // PIECES), cols // PIECES)
+        return remote(theirs.at[:, n], d2d.at[0, :, n], first_send.at[k], first_recv.at[k], sibling)
 
     n_steps = jnp.where(is_outer, max(STEPS[True]) + 1, max(STEPS[False]) + 1)
     most = max(max(STEPS[True]), max(STEPS[False])) + 1
@@ -191,9 +195,10 @@
             w_copy(2, 2 * (k - PIECES)).start()
             w_copy(2, 2 * (k - PIECES) + 1).start()
 
+    load(jnp.int32(0))
     for copy in x_copies(jnp.int32(0)):
         copy.start()
-    for k in range(AHEAD):
+    for k in range(1, AHEAD):
         load(jnp.int32(k))
 
     barrier = pltpu.get_barrier_semaphore()
@@ -297,13 +302,22 @@
             def part(k, carry):
                 w_copy(2, k).wait()
                 term(pl.ds(pl.multiple_of(k * d_cols, d_cols), d_cols))
+                first_copy(k).start()
                 return carry
 
             lax.fori_loop(0, PIECES, part, None)
 
         @pl.when(s > 0)
         def _():
-            d2d_copy(s - 1).wait_send()
+            @pl.when(s == 1)
+            def _():
+                for k in range(PIECES):
+                    first_copy(k).wait_send()
+
+            @pl.when(s > 1)
+            def _():
+                d2d_copy(s - 1).wait_send()
+
             n_cols = cols
 
             def part(k, carry):
@@ -311,14 +325,18 @@
                 return carry
 
             lax.fori_loop(0, cols // n_cols, part, None)
-
-        d2d_copy(s).start()
+            d2d_copy(s).start()
 
     def round_(i, carry):
         r = i - 1
         s = r + 1
 
-        @pl.when((r >= 0) & (r < n_steps))
+        @pl.when(r == 0)
+        def _():
+            for k in range(PIECES):
+                first_copy(k).wait_recv()
+
+        @pl.when((r > 0) & (r < n_steps))
         def _():
             d2d_copy(r).wait_recv()
 
@@ -407,6 +425,8 @@
             pltpu.VMEM((N_EXTRA, half, cols), BF16),
             dma((3, PIECES)),
             dma((2 * SLOT,)),
+            dma((PIECES,)),
+            dma((PIECES,)),
             dma((1,)),
             dma((2,)),
             dma((3, 2, SUBS)),

time: 197 us -> 197 us (level)
  no operation moved by 1% of the time
where the time goes in v4:
time: 197 us
  Pallas kernels  197 us (100%)
    pallas_call x1, Pallas kernels, mlp(): pl.pallas_call(block_kernel, out_shape=pltpu.VMEM((rows, cols), BF16), in...  189 us
    pallas_call x1, Pallas kernels, mlp(): pl.pallas_call(functools.partial(copy_out_kernel, parts), out_shape=jax.S...  7.23 us

profile of v4, /device:TPU:0, one launch (start us, length us, event | category | flops | bytes accessed | tf_op | source)
XLA Modules:
  0.0 196.7 jit_solution(2061584261904328383)
XLA Ops:
  0.0 189.4 %mlp_trees.1.src = bf16[2048,5120]{1,0:T(8,128)(2,1)S(1)} custom-call(bf16[2048,5120]{1,0:T(8,128)(2,1)} %x.1, bf16[5120,1024]{1,0:T(8,128)(2,1)} %wg.1, bf16[5120,1024]{1,0:T(8,128)(2,1)} %wu.1, bf16[1024,5120]{1,0:T(8,128)(2,1)} %wd.1), custom_call_target="tpu_custom_call" | custom-call | flops 64424509440 | bytes 52428800 | tf_op jit(solution)/shard_map/mlp_trees/pallas_call | solution.py:410
  189.4 7.2 %copy_out.1 = bf16[2048,5120]{1,0:T(8,128)(2,1)} custom-call(bf16[2048,5120]{1,0:T(8,128)(2,1)S(1)} %mlp_trees.1.src), custom_call_target="tpu_custom_call" | custom-call | tf_op jit(solution)/shard_map/copy_out/pallas_call | solution.py:447
